TPU v7x, 256 devices: a 8x8x2 block of a 8x8x16 slice. The times are simulated.
256 devices in a mesh: groups: 2 (over z), patch: 128 (over x, y, core).
Axes of the slice: x: 8, y: 8, z: 2, core: 2. Of those that a mesh axis runs over, the one named last changes fastest.
The devices are a block of a 8x8x16 slice.
Arguments:
- grid_latents: bfloat16 [262144, 512], P(('groups', 'patch')), parts along dimension 0, may hold values from -6 to 6
- mesh_latents: bfloat16 [131072, 512], P(('groups', 'patch')), parts along dimension 0, may hold values from -6 to 6
- enc_send: int32 [5120, 128], P(('groups', 'patch')), parts along dimension 0, may hold values from 0 to 1023
- enc_recv: int32 [5120, 128], P(('groups', 'patch')), parts along dimension 0, may hold values from 0 to 512, as said below
- neighbours: int32 [131072, 32], P(('groups', 'patch')), parts along dimension 0, may hold values from 0 to 65535, as said below
- enc_grid_w: bfloat16 [512, 512], replicated, may hold values from -0.25 to 0.25
- enc_bias: float32 [512], replicated, may hold values from -4 to 4
- enc_mesh_w: bfloat16 [512, 512], replicated, may hold values from -0.25 to 0.25
- enc_msg_w: bfloat16 [512, 512], replicated, may hold values from -0.25 to 0.25
- upd_agg_w: bfloat16 [512, 512], replicated, may hold values from -0.25 to 0.25
- upd_mesh_w: bfloat16 [512, 512], replicated, may hold values from -0.25 to 0.25
- upd_out_w: bfloat16 [512, 512], replicated, may hold values from -0.25 to 0.25
- norm_gain: float32 [512], replicated, may hold values from 0.1 to 1.9
- query_w: bfloat16 [512, 512], replicated, may hold values from -0.25 to 0.25
- key_w: bfloat16 [512, 512], replicated, may hold values from -0.25 to 0.25
- value_w: bfloat16 [512, 512], replicated, may hold values from -0.25 to 0.25
- out_w: bfloat16 [512, 512], replicated, may hold values from -0.25 to 0.25
- ffn_gain: float32 [512], replicated, may hold values from 0.1 to 1.9
- ffn_in_w: bfloat16 [512, 2048], replicated, may hold values from -0.25 to 0.25
- ffn_out_w: bfloat16 [2048, 512], replicated, may hold values from -0.125 to 0.125
Outputs:
- result: bfloat16 [131072, 512], P(('groups', 'patch')), parts along dimension 0
There are 2 independent parts, one for each index of `groups`. A program takes and returns all parts, laid end to end along the dimension named above; an argument that names none is the same for every part. Nothing has to cross between parts.
Inputs may be any that keep to these rules, and one draw needn't show every extreme that they name: `enc_recv`: in each band's slots for one owner, the used edges come first and the rest hold 512; the first and last bands fill all their slots. `neighbours`: neighbour 0 of a node is the node itself; every neighbour's owner is within 2 patch indices of the node's owner, wrapping around.
All inputs are finite; a program needn't handle non-finite values.
Results may differ from a plain program's by a relative error of at most 0.006.
The roundings to bfloat16 on the way count: a program that leaves them out, or rounds other values in their place, can miss the bound.
Values may be sent and summed in bfloat16 or wider, within the bound.
A program may use at most 256 MiB of HBM per device.

v0:
```python
import functools
import math

import jax
import jax.numpy as jnp
from jax import lax
from jax.experimental import pallas as pl
from jax.experimental.pallas import tpu as pltpu
from jax.sharding import PartitionSpec as P

HEADS = 4
REACH = 2
LANES = 128
CHUNK = 256

NORM_EPS = 1e-05
HEAD_EPS = 1e-06

OWN, SIB, OTH, FW, NF = range(5)
DELTA = {OWN: 0, SIB: 1, OTH: -1, FW: 2, NF: -2}
MIRROR = {SIB: SIB, OTH: OTH, FW: NF, NF: FW}

EDGE_SEND = [(FW, 0), (NF, 0), (FW, 1), (NF, 1), (OTH, 0), (OTH, 1), (SIB, 0), (SIB, 1), (OWN, 0), (OWN, 1)]
EDGE_USE = [(OWN, 0), (OWN, 1), (SIB, 0), (SIB, 1), (NF, 0), (FW, 0), (NF, 1), (FW, 1), (OTH, 0), (OTH, 1)]
EDGE_SLOT = {key: slot for slot, key in enumerate(EDGE_USE)}
NODE_USE = [(OWN, 0), (OWN, 1), (SIB, 0), (SIB, 1), (NF, 0), (FW, 0), (OTH, 0), (NF, 1), (FW, 1), (OTH, 1)]
NODE_SLOT = {key: slot for slot, key in enumerate(NODE_USE)}

f32 = jnp.float32
bf16 = jnp.bfloat16
i32 = jnp.int32


def dot(a, b):
    return jnp.dot(a, b, preferred_element_type=f32)


def dot_last(a, b):
    return lax.dot_general(a, b, (((1,), (1,)), ((), ())), preferred_element_type=f32)


def silu(x):
    half = 0.5 * x
    return half * jnp.tanh(half) + half


def flag(mask):
    return jnp.where(mask, 1.0, 0.0).astype(bf16)


def kernel(
    count,
    grid_hbm, mesh_hbm, send_ref, recv_ref, neigh_ref,
    grid_w_hbm, bias_ref, mesh_w_hbm, msg_w_hbm, upd_agg_hbm, upd_mesh_hbm, upd_out_hbm,
    gain_ref, query_hbm, key_hbm, value_hbm, out_w_hbm, ffn_gain_ref, ffn_in_hbm, ffn_out_hbm,
    result_ref,
    grid_v, mesh_v, grid_w, mesh_w, msg_w, upd_agg, upd_mesh, upd_out, query_w, key_w, value_w, out_w, ffn_in, ffn_out,
    projected, receiver, base, summed, encoded, edges, nodes, counts, queries, values, mixed,
    send_cols, land_cols, land_rows, stage, land_send, land_recv, hi_tiled, lo_tiled,
    load_sem, ls_sem, lr_sem, es_sem, er_sem, ns_sem, nr_sem,
):
    me = lax.axis_index("patch")
    sign = 1 - 2 * (me % 2)
    device = {role: (me + sign * DELTA[role] + count) % count for role in DELTA}
    block_row = {role: 4 * (sign * DELTA[role] + REACH) for role in DELTA}
    rows = mesh_v.shape[0]

    def load(index, src, dst):
        copy = pltpu.make_async_copy(src, dst, load_sem.at[index])
        copy.start()
        return copy

    def remote(src, dst, send_sem, recv_sem, role):
        return pltpu.make_async_remote_copy(
            src_ref=src, dst_ref=dst, send_sem=send_sem, recv_sem=recv_sem,
            device_id={"patch": device[role]}, device_id_type=pl.DeviceIdType.MESH,
        )

    pairs = [
        (grid_hbm, grid_v), (grid_w_hbm, grid_w), (mesh_hbm, mesh_v), (mesh_w_hbm, mesh_w), (msg_w_hbm, msg_w),
        (upd_mesh_hbm, upd_mesh), (upd_agg_hbm, upd_agg), (upd_out_hbm, upd_out), (query_hbm, query_w),
        (key_hbm, key_w), (value_hbm, value_w), (out_w_hbm, out_w), (ffn_in_hbm, ffn_in), (ffn_out_hbm, ffn_out),
    ]
    loads = [load(index, src, dst) for index, (src, dst) in enumerate(pairs)]

    barrier = pltpu.get_barrier_semaphore()
    for role in (SIB, OTH, FW, NF):
        pl.semaphore_signal(
            barrier, inc=1, device_id={"patch": device[role]}, device_id_type=pl.DeviceIdType.MESH
        )

    land_send[...] = jnp.zeros_like(land_send)
    stage[...] = jnp.zeros_like(stage)
    for role in DELTA:
        for j in range(4):
            land_send[role, j : j + 1, :] = recv_ref[pl.ds(block_row[role] + j, 1), :]
    for k, (role, half) in enumerate(EDGE_SEND):
        for j in range(2):
            stage[2 * k + j : 2 * k + j + 1, :] = send_ref[pl.ds(block_row[role] + 2 * half + j, 1), :]

    pl.semaphore_wait(barrier, 4)
    land_copies = []
    for role in (SIB, OTH, FW, NF):
        copy = remote(
            land_send.at[role], land_recv.at[MIRROR[role]], ls_sem.at[role - 1], lr_sem.at[MIRROR[role] - 1], role
        )
        copy.start()
        land_copies.append(copy)

    turned = stage[...].T
    for b in range(20):
        send_cols[b] = jnp.broadcast_to(turned[:, b : b + 1], (LANES, LANES))

    lane = lax.broadcasted_iota(i32, (CHUNK, LANES), 1)

    def onehot(cols, k, width):
        col = jnp.concatenate([cols[2 * k], cols[2 * k + 1]], axis=0)
        return jnp.concatenate([flag(col == lane + LANES * t) for t in range(width // LANES)], axis=1)

    loads[0].wait()
    loads[1].wait()

    def project(t, carry):
        at = pl.ds(pl.multiple_of(t * CHUNK, CHUNK), CHUNK)
        projected[at, :] = (dot(grid_v[at, :], grid_w[...]) + bias_ref[...]).astype(bf16)
        return carry

    lax.fori_loop(0, grid_v.shape[0] // CHUNK, project, 0)

    def edge_copy(k):
        role, half = EDGE_SEND[k]
        slot = EDGE_SLOT[(MIRROR[role], half)]
        return remote(edges.at[10 + k], edges.at[slot], es_sem.at[k], er_sem.at[slot - 2], role)

    def pick(k, carry):
        chosen = onehot(send_cols, k, grid_v.shape[0])
        edges[(10 + k) % 18] = dot(chosen, projected[...]).astype(bf16)
        for index in range(8):
            @pl.when(k == index)
            def _():
                edge_copy(index).start()
        return carry

    lax.fori_loop(0, 10, pick, 0)

    loads[2].wait()
    loads[3].wait()
    loads[5].wait()

    def prepare(t, carry):
        at = pl.ds(pl.multiple_of(t * CHUNK, CHUNK), CHUNK)
        latents = mesh_v[at, :]
        receiver[at, :] = dot(latents, mesh_w[...]).astype(bf16)
        base[at, :] = dot(latents, upd_mesh[...])
        summed[at, :] = jnp.zeros((CHUNK, summed.shape[1]), f32)
        return carry

    lax.fori_loop(0, rows // CHUNK, prepare, 0)

    for role in (SIB, OTH, FW, NF):
        remote(land_send.at[role], land_recv.at[role], ls_sem.at[role - 1], lr_sem.at[role - 1], role).wait_recv()
    for i, (role, half) in enumerate(EDGE_USE):
        source = land_send if role == OWN else land_recv
        for j in range(2):
            row = source[role, 2 * half + j : 2 * half + j + 1, :]
            land_rows[2 * i + j] = row
            stage[2 * i + j : 2 * i + j + 1, :] = row
    landed = stage[...].T
    for b in range(20):
        land_cols[b] = jnp.broadcast_to(landed[:, b : b + 1], (LANES, LANES))
    loads[4].wait()

    def use_edges(i):
        receiver_rows = dot(onehot(land_cols, i, rows), receiver[...])
        active = silu(edges[i].astype(f32) + receiver_rows).astype(bf16)
        message = dot(active, msg_w[...]).astype(bf16)
        landing = jnp.concatenate([land_rows[2 * i], land_rows[2 * i + 1]], axis=1)
        scatter = flag(lax.broadcasted_iota(i32, (rows, CHUNK), 0) == landing)
        summed[...] += dot(scatter, message)

    def own_edges(i, carry):
        use_edges(i)
        return carry

    lax.fori_loop(0, 2, own_edges, 0)

    neigh = neigh_ref[...]
    owner = lax.div(neigh, i32(rows))
    row = lax.rem(neigh, i32(rows))
    step = lax.rem((owner - me) * sign + 2 * count, i32(count))
    half = lax.div(row, i32(CHUNK))
    near = jnp.where(step == 0, half, 2 + half)
    far = jnp.where(step == count - 2, 4, jnp.where(step == 2, 5, 6)) + 3 * half
    slot = jnp.where(step <= 1, near, far)
    high = 2 * slot + lax.rem(lax.div(row, i32(LANES)), i32(2))
    low = lax.rem(row, i32(LANES))
    links = neigh.shape[1]
    spread = flag(
        lax.rem(lax.broadcasted_iota(i32, (links, LANES), 1), i32(links))
        == lax.broadcasted_iota(i32, (links, LANES), 0)
    )
    hi_tiled[...] = dot(high.astype(f32).astype(bf16), spread)
    lo_tiled[...] = dot(low.astype(f32).astype(bf16), spread)
    sub8 = lax.broadcasted_iota(i32, (8, LANES), 0)
    piece = lax.div(lax.broadcasted_iota(i32, (8, LANES), 1), i32(links))
    first = piece == sub8
    second = piece + LANES // links == sub8
    low_id = lax.broadcasted_iota(i32, (LANES, 2 * LANES), 0).astype(f32)

    def count_group(g, carry):
        at = pl.ds(pl.multiple_of(8 * g, 8), 8)
        h8, l8 = hi_tiled[at, :], lo_tiled[at, :]
        key = jnp.concatenate([jnp.where(first, h8, -1.0), jnp.where(second, h8, -1.0)], axis=1)
        by_high = jnp.concatenate([jnp.where(key == float(v), 1.0, 0.0) for v in range(20)], axis=0).astype(bf16)
        low_row = jnp.concatenate(
            [
                jnp.sum(jnp.where(first, l8, 0.0), axis=0, keepdims=True),
                jnp.sum(jnp.where(second, l8, 0.0), axis=0, keepdims=True),
            ],
            axis=1,
        )
        by_low = flag(low_id == low_row)
        found = dot_last(by_high, by_low)
        for v in range(20):
            counts[v // 2, at, (v % 2) * LANES : (v % 2 + 1) * LANES] = found[8 * v : 8 * v + 8, :]
        return carry

    lax.fori_loop(0, rows // 8, count_group, 0, unroll=2)

    def far_edges(i, carry):
        pltpu.make_async_remote_copy(
            src_ref=edges.at[i], dst_ref=edges.at[i], send_sem=es_sem.at[0], recv_sem=er_sem.at[i - 2],
            device_id={"patch": device[SIB]}, device_id_type=pl.DeviceIdType.MESH,
        ).wait_recv()
        use_edges(i)
        return carry

    lax.fori_loop(2, 10, far_edges, 0)

    for index in (6, 7, 8):
        loads[index].wait()

    def node_copy(index, role, half):
        slot = NODE_SLOT[(MIRROR[role], half)]
        return remote(
            nodes.at[NODE_SLOT[(OWN, half)]], nodes.at[slot], ns_sem.at[index], nr_sem.at[slot - 2], role
        )

    head = rows // HEADS
    query_scale = math.log2(math.e) / math.sqrt(head)

    def unit(x, scale):
        parts = []
        for h in range(HEADS):
            part = x[:, h * head : (h + 1) * head]
            square = jnp.mean(part * part, axis=-1, keepdims=True)
            parts.append((part * (lax.rsqrt(square + HEAD_EPS) * scale)).astype(bf16))
        return jnp.concatenate(parts, axis=1)

    def rms_scale(x, gain):
        square = jnp.mean(x * x, axis=-1, keepdims=True)
        return (x * lax.rsqrt(square + NORM_EPS) * gain).astype(bf16)

    node_copies = []
    for c in range(2):
        at = slice(c * CHUNK, (c + 1) * CHUNK)
        update = silu(dot(summed[at, :].astype(bf16), upd_agg[...]) + base[at, :]).astype(bf16)
        latent = mesh_v[at, :].astype(f32) + dot(update, upd_out[...])
        encoded[at, :] = latent
        nodes[c] = rms_scale(latent, gain_ref[...])
        for index, role in enumerate((NF, FW, SIB)):
            copy = node_copy(3 * c + index, role, c)
            copy.start()
            node_copies.append(copy)
    for c in range(2):
        at = slice(c * CHUNK, (c + 1) * CHUNK)
        queries[at, :] = unit(dot(nodes[c], query_w[...]), query_scale)
    mixed[...] = jnp.zeros_like(mixed)
    values[...] = jnp.ones_like(values)
    loads[9].wait()
    loads[10].wait()

    def pass_on(half):
        source = NODE_SLOT[(FW, half)]
        slot = NODE_SLOT[(OTH, half)]
        return remote(nodes.at[source], nodes.at[slot], ns_sem.at[6 + half], nr_sem.at[slot - 2], SIB)

    def arrived(slot):
        remote(nodes.at[slot], nodes.at[slot], ns_sem.at[0], nr_sem.at[slot - 2], SIB).wait_recv()

    def attend(i, carry):
        for role, half in NODE_USE[2:]:
            index = NODE_SLOT[(role, half)]
            if role == FW:
                continue

            @pl.when(i == index)
            def _():
                if role == NF:
                    arrived(NODE_SLOT[(FW, half)])
                    pass_on(half).start()
                arrived(index)

        features = nodes[i]
        keys = unit(dot(features, key_w[...]), 1.0)
        value = dot(features, value_w[...]).astype(bf16)
        for h in range(HEADS):
            values[:, 2 * h * head : (2 * h + 1) * head] = value[:, h * head : (h + 1) * head]
        for t in range(rows // CHUNK):
            at = slice(t * CHUNK, (t + 1) * CHUNK)
            often = counts[i, at, :]
            for h in range(HEADS):
                cols = slice(h * head, (h + 1) * head)
                score = dot_last(queries[at, cols], keys[:, cols])
                weight = (jnp.exp2(score) * often).astype(bf16)
                wide = slice(2 * h * head, 2 * (h + 1) * head)
                mixed[at, wide] += dot(weight, values[:, wide])
        return carry

    lax.fori_loop(0, 10, attend, 0)

    for index in (11, 12, 13):
        loads[index].wait()

    def finish(t, carry):
        at = pl.ds(pl.multiple_of(t * CHUNK, CHUNK), CHUNK)
        attended = jnp.concatenate(
            [
                mixed[at, 2 * h * head : (2 * h + 1) * head] / mixed[at, (2 * h + 1) * head : 2 * (h + 1) * head]
                for h in range(HEADS)
            ],
            axis=1,
        ).astype(bf16)
        hidden = encoded[at, :] + dot(attended, out_w[...])
        normed = rms_scale(hidden, ffn_gain_ref[...])
        for c in range(ffn_in.shape[1] // 512):
            cols = slice(512 * c, 512 * (c + 1))
            expanded = silu(dot(normed, ffn_in[:, cols])).astype(bf16)
            hidden = hidden + dot(expanded, ffn_out[cols, :])
        result_ref[at, :] = hidden.astype(bf16)
        return carry

    lax.fori_loop(0, rows // CHUNK, finish, 0)

    for copy in land_copies + [edge_copy(k) for k in range(8)] + node_copies + [pass_on(0), pass_on(1)]:
        copy.wait_send()


def shards(
    grid_latents, mesh_latents, enc_send, enc_recv, neighbours,
    enc_grid_w, enc_bias, enc_mesh_w, enc_msg_w, upd_agg_w, upd_mesh_w, upd_out_w,
    norm_gain, query_w, key_w, value_w, out_w, ffn_gain, ffn_in_w, ffn_out_w,
):
    count = lax.axis_size("patch")
    rows, width = mesh_latents.shape
    any_spec = pl.BlockSpec(memory_space=pl.ANY)
    vmem_spec = pl.BlockSpec(memory_space=pltpu.VMEM)
    square = pltpu.VMEM((width, width), bf16)
    args = (
        grid_latents, mesh_latents, enc_send, enc_recv, neighbours,
        enc_grid_w, enc_bias[None, :], enc_mesh_w, enc_msg_w, upd_agg_w, upd_mesh_w, upd_out_w,
        norm_gain[None, :], query_w, key_w, value_w, out_w, ffn_gain[None, :], ffn_in_w, ffn_out_w,
    )
    in_vmem = {2, 3, 4, 6, 12, 17}
    return pl.pallas_call(
        functools.partial(kernel, count),
        out_shape=jax.ShapeDtypeStruct((rows, width), bf16),
        in_specs=[vmem_spec if index in in_vmem else any_spec for index in range(len(args))],
        out_specs=vmem_spec,
        scratch_shapes=[
            pltpu.VMEM(grid_latents.shape, bf16),
            pltpu.VMEM((rows, width), bf16),
            *([square] * 10),
            pltpu.VMEM(ffn_in_w.shape, bf16),
            pltpu.VMEM(ffn_out_w.shape, bf16),
            pltpu.VMEM(grid_latents.shape, bf16),
            pltpu.VMEM((rows, width), bf16),
            pltpu.VMEM((rows, width), f32),
            pltpu.VMEM((rows, width), f32),
            pltpu.VMEM((rows, width), f32),
            pltpu.VMEM((18, CHUNK, width), bf16),
            pltpu.VMEM((10, CHUNK, width), bf16),
            pltpu.VMEM((10, rows, CHUNK), f32),
            pltpu.VMEM((rows, width), bf16),
            pltpu.VMEM((CHUNK, 2 * width), bf16),
            pltpu.VMEM((rows, 2 * width), f32),
            pltpu.VMEM((20, LANES, LANES), i32),
            pltpu.VMEM((20, LANES, LANES), i32),
            pltpu.VMEM((20, 1, LANES), i32),
            pltpu.VMEM((LANES, LANES), i32),
            pltpu.VMEM((5, 8, LANES), i32),
            pltpu.VMEM((5, 8, LANES), i32),
            pltpu.VMEM((rows, LANES), f32),
            pltpu.VMEM((rows, LANES), f32),
            pltpu.SemaphoreType.DMA((14,)),
            pltpu.SemaphoreType.DMA((4,)),
            pltpu.SemaphoreType.DMA((4,)),
            pltpu.SemaphoreType.DMA((8,)),
            pltpu.SemaphoreType.DMA((8,)),
            pltpu.SemaphoreType.DMA((8,)),
            pltpu.SemaphoreType.DMA((8,)),
        ],
        compiler_params=pltpu.CompilerParams(
            collective_id=0, has_side_effects=True, vmem_limit_bytes=60 * 2**20
        ),
        name="encode_attend",
    )(*args)


def solution(mesh):
    split = P(("groups", "patch"), None)
    in_specs = (split,) * 5 + (P(),) * 15
    return jax.shard_map(shards, mesh=mesh, in_specs=in_specs, out_specs=split, check_vma=False)
```

profile of v0, /device:TPU:513, one launch (start us, length us, event | category | flops | bytes accessed | tf_op | source)
XLA Modules:
  0.0 75.3 jit_solution(11279721004243344396)
XLA Ops:
  0.0 1.7 %copy.21.neigh_ref = s32[512,32]{1,0:T(8,128)} copy(s32[512,32]{0,1:T(8,128)} %param.24) | data formatting | bytes 131072 | tf_op args[4]
  1.7 71.8 %encode_attend.1 = bf16[512,512]{1,0:T(8,128)(2,1)} custom-call(bf16[1024,512]{1,0:T(8,128)(2,1)} %grid_hbm.1, bf16[512,512]{1,0:T(8,128)(2,1)} %mesh_hbm.1, s32[20,128]{1,0:T(8,128)} %send_ref.1, s32[20,128]{1,0:T(8,128)} %recv_ref.1, s32[512,32]{1,0:T(8,128)} %copy.21.neigh_ref, bf16[512,512]{1,0:T(8,128)(2,1)} %grid_w_hbm.1, f32[1,512]{1,0:T(1,128)} %bitcast.3, ...), custom_call_target="tpu_custom_call" | custom-call | tf_op jit(solution)/shard_map/encode_attend/pallas_call | solution.py:365
  73.5 1.9 %copy.23 = bf16[512,512]{1,0:T(8,128)(2,1)} copy(bf16[512,512]{1,0:T(8,128)(2,1)} %encode_attend.1) | data formatting | bytes 1048576
where the time goes:
time: 75.5 us; the launch traced here: 75.3 us
  Pallas kernels  71.8 us (95%)
  local copies, waits for them, and re-layouts  3.54 us (5%)
    pallas_call x1, Pallas kernels, shards(): pl.pallas_call(functools.partial(kernel, count), out_shape=jax.ShapeDtype...  71.8 us
    unnamed x2, local copies, waits for them, and re-layouts  3.54 us

commit v1 on v0

v1 whole, which is shorter than its diff:
```python
import functools
import math

import jax
import jax.numpy as jnp
from jax import lax
from jax.experimental import pallas as pl
from jax.experimental.pallas import tpu as pltpu
from jax.sharding import PartitionSpec as P

HEADS = 4
REACH = 2
LANES = 128
CHUNK = 256

NORM_EPS = 1e-05
HEAD_EPS = 1e-06

OWN, SIB, OTH, FW, NF = range(5)
DELTA = {OWN: 0, SIB: 1, OTH: -1, FW: 2, NF: -2}
MIRROR = {SIB: SIB, OTH: OTH, FW: NF, NF: FW}

EDGE_SEND = [(FW, 0), (NF, 0), (FW, 1), (NF, 1), (OTH, 0), (OTH, 1), (SIB, 0), (SIB, 1), (OWN, 0), (OWN, 1)]
EDGE_USE = [(OWN, 0), (OWN, 1), (SIB, 0), (SIB, 1), (NF, 0), (FW, 0), (NF, 1), (FW, 1), (OTH, 0), (OTH, 1)]
EDGE_SLOT = {key: slot for slot, key in enumerate(EDGE_USE)}
NODE_USE = (
    [(OWN, q) for q in range(4)] + [(SIB, q) for q in range(4)]
    + [(FW, 0), (FW, 1), (OTH, 0), (OTH, 1), (FW, 2), (NF, 0)]
    + [(FW, 3), (OTH, 2), (OTH, 3), (NF, 1), (NF, 2), (NF, 3)]
)
NODE_SLOT = {key: slot for slot, key in enumerate(NODE_USE)}

f32 = jnp.float32
bf16 = jnp.bfloat16
i32 = jnp.int32


def dot(a, b):
    return jnp.dot(a, b, preferred_element_type=f32)


def dot_last(a, b):
    return lax.dot_general(a, b, (((1,), (1,)), ((), ())), preferred_element_type=f32)


def dot_first(a, b):
    return lax.dot_general(a, b, (((0,), (0,)), ((), ())), preferred_element_type=f32)


def silu(x):
    half = 0.5 * x
    return half * jnp.tanh(half) + half


def flag(mask):
    return jnp.where(mask, 1.0, 0.0).astype(bf16)


def kernel(
    count,
    grid_hbm, mesh_hbm, send_hbm, recv_hbm, neigh_hbm,
    grid_w_hbm, bias_hbm, mesh_w_hbm, msg_w_hbm, upd_agg_hbm, upd_mesh_hbm, upd_out_hbm,
    gain_hbm, query_hbm, key_hbm, value_hbm, out_w_hbm, ffn_gain_hbm, ffn_in_hbm, ffn_out_hbm,
    result_ref,
    grid_v, mesh_v, send_ref, recv_ref, neigh_ref, bias_ref, gain_ref, ffn_gain_ref, grid_w, mesh_w, msg_w, upd_agg, upd_mesh, upd_out, query_w, key_w, value_w, out_w, ffn_in, ffn_out,
    projected, receiver, received, base, summed, encoded, edges, nodes, counts, queries, values, mixed,
    send_cols, land_cols, land_rows, stage, land_send, land_recv, hi_tiled, lo_rows, expanded,
    load_sem, ls_sem, lr_sem, es_sem, er_sem, ns_sem, nr_sem,
):
    me = lax.axis_index("patch")
    sign = 1 - 2 * (me % 2)
    device = {role: (me + sign * DELTA[role] + count) % count for role in DELTA}
    block_row = {role: 4 * (sign * DELTA[role] + REACH) for role in DELTA}
    rows = mesh_v.shape[0]

    def load(index, src, dst):
        copy = pltpu.make_async_copy(src, dst, load_sem.at[index])
        copy.start()
        return copy

    def remote(src, dst, send_sem, recv_sem, role):
        return pltpu.make_async_remote_copy(
            src_ref=src, dst_ref=dst, send_sem=send_sem, recv_sem=recv_sem,
            device_id={"patch": device[role]}, device_id_type=pl.DeviceIdType.MESH,
        )

    pairs = [
        (send_hbm, send_ref), (recv_hbm, recv_ref), (bias_hbm, bias_ref), (grid_hbm, grid_v), (grid_w_hbm, grid_w), (mesh_hbm, mesh_v), (mesh_w_hbm, mesh_w), (msg_w_hbm, msg_w),
        (upd_mesh_hbm, upd_mesh), (upd_agg_hbm, upd_agg), (upd_out_hbm, upd_out), (query_hbm, query_w),
        (gain_hbm, gain_ref), (ffn_gain_hbm, ffn_gain_ref), (neigh_hbm, neigh_ref), (key_hbm, key_w), (value_hbm, value_w), (out_w_hbm, out_w), (ffn_in_hbm, ffn_in), (ffn_out_hbm, ffn_out),
    ]
    loads = {id(dst): load(index, src, dst) for index, (src, dst) in enumerate(pairs[:5])}

    def wait_for(*refs):
        for ref in refs:
            loads[id(ref)].wait()

    barrier = pltpu.get_barrier_semaphore()
    for role in (SIB, OTH, FW, NF):
        pl.semaphore_signal(
            barrier, inc=1, device_id={"patch": device[role]}, device_id_type=pl.DeviceIdType.MESH
        )

    wait_for(send_ref, recv_ref)

    land_send[...] = jnp.zeros_like(land_send)
    stage[...] = jnp.zeros_like(stage)
    for role in DELTA:
        for j in range(4):
            land_send[role, j : j + 1, :] = recv_ref[pl.ds(block_row[role] + j, 1), :]
    for k, (role, half) in enumerate(EDGE_SEND):
        for j in range(2):
            stage[2 * k + j : 2 * k + j + 1, :] = send_ref[pl.ds(block_row[role] + 2 * half + j, 1), :]

    land_copies = [
        remote(land_send.at[role], land_recv.at[MIRROR[role]], ls_sem.at[role - 1], lr_sem.at[MIRROR[role] - 1], role)
        for role in (SIB, OTH, FW, NF)
    ]

    turned = stage[...].T
    for b in range(20):
        send_cols[b] = jnp.broadcast_to(turned[:, b : b + 1], (LANES, LANES))

    lane = lax.broadcasted_iota(i32, (CHUNK, LANES), 1)

    def onehot(cols, k, width):
        col = jnp.concatenate([cols[2 * k], cols[2 * k + 1]], axis=0)
        return jnp.concatenate([flag(col == lane + LANES * t) for t in range(width // LANES)], axis=1)

    with jax.named_scope("wait_grid"):
        wait_for(grid_v, grid_w, bias_ref)
    loads |= {id(dst): load(index + 5, src, dst) for index, (src, dst) in enumerate(pairs[5:])}

    def project(t, carry):
        at = pl.ds(pl.multiple_of(t * rows, rows), rows)
        projected[at, :] = (dot(grid_v[at, :], grid_w[...]) + bias_ref[...]).astype(bf16)
        return carry

    with jax.named_scope("project"):
        lax.fori_loop(0, grid_v.shape[0] // rows, project, 0)

    def edge_copy(k):
        role, half = EDGE_SEND[k]
        slot = EDGE_SLOT[(MIRROR[role], half)]
        return remote(edges.at[10 + k], edges.at[slot], es_sem.at[k], er_sem.at[slot - 2], role)

    def pick(k, carry):
        chosen = onehot(send_cols, k, grid_v.shape[0])
        edges[(10 + k) % 18] = dot(chosen, projected[...]).astype(bf16)

        @pl.when(k == 0)
        def _():
            pl.semaphore_wait(barrier, 4)
            for copy in land_copies:
                copy.start()

        for index in range(8):
            @pl.when(k == index)
            def _():
                edge_copy(index).start()
        return carry

    with jax.named_scope("pick"):
        lax.fori_loop(0, 10, pick, 0)

    wait_for(mesh_v, mesh_w, upd_mesh)

    def prepare(t, carry):
        at = pl.ds(pl.multiple_of(t * CHUNK, CHUNK), CHUNK)
        latents = mesh_v[at, :]
        receiver[at, :] = dot(latents, mesh_w[...]).astype(bf16)
        base[at, :] = dot(latents, upd_mesh[...])
        summed[at, :] = jnp.zeros((CHUNK, summed.shape[1]), f32)
        return carry

    with jax.named_scope("prepare"):
        lax.fori_loop(0, rows // CHUNK, prepare, 0)

    for role in (SIB, OTH, FW, NF):
        remote(land_send.at[role], land_recv.at[role], ls_sem.at[role - 1], lr_sem.at[role - 1], role).wait_recv()
    for i, (role, half) in enumerate(EDGE_USE):
        source = land_send if role == OWN else land_recv
        for j in range(2):
            row = source[role, 2 * half + j : 2 * half + j + 1, :]
            land_rows[2 * i + j] = row
            stage[2 * i + j : 2 * i + j + 1, :] = row
    landed = stage[...].T
    for b in range(20):
        land_cols[b] = jnp.broadcast_to(landed[:, b : b + 1], (LANES, LANES))
    wait_for(msg_w)

    def receive(i, carry):
        received[i] = dot(onehot(land_cols, i, rows), receiver[...]).astype(bf16)
        return carry

    def use_edges(i):
        active = silu(edges[i].astype(f32) + received[i].astype(f32)).astype(bf16)
        message = dot(active, msg_w[...]).astype(bf16)
        landing = jnp.concatenate([land_rows[2 * i], land_rows[2 * i + 1]], axis=1)
        scatter = flag(lax.broadcasted_iota(i32, (rows, CHUNK), 0) == landing)
        summed[...] += dot(scatter, message)

    def own_edges(i, carry):
        use_edges(i)
        return carry

    with jax.named_scope("receive"):
        lax.fori_loop(0, 10, receive, 0)
    with jax.named_scope("own_edges"):
        lax.fori_loop(0, 2, own_edges, 0)

    wait_for(neigh_ref)
    neigh = neigh_ref[...]
    owner = lax.div(neigh, i32(rows))
    row = lax.rem(neigh, i32(rows))
    step = lax.rem((owner - me) * sign + 2 * count, i32(count))
    quarter = lax.div(row, i32(LANES))
    far = jnp.zeros_like(quarter)
    for role, offset in ((FW, 2), (NF, count - 2), (OTH, count - 1)):
        for q in range(4):
            far = jnp.where((step == offset) & (quarter == q), NODE_SLOT[(role, q)], far)
    high = jnp.where(step <= 1, quarter + 4 * step, far)
    low = lax.rem(row, i32(LANES))
    links = neigh.shape[0]
    spread = flag(
        lax.rem(lax.broadcasted_iota(i32, (links, LANES), 1), i32(links))
        == lax.broadcasted_iota(i32, (links, LANES), 0)
    )
    hi_tiled[...] = dot_first(high.astype(f32).astype(bf16), spread)
    lo_tiled = dot_first(low.astype(f32).astype(bf16), spread)
    place = lax.rem(lax.broadcasted_iota(i32, (rows, LANES), 0), i32(8))
    node_piece = lax.div(lax.broadcasted_iota(i32, (rows, LANES), 1), i32(links))
    alone = jnp.concatenate(
        [
            jnp.where(node_piece == place, lo_tiled, 0.0).astype(bf16),
            jnp.where(node_piece + LANES // links == place, lo_tiled, 0.0).astype(bf16),
        ],
        axis=1,
    )
    group = flag(
        lax.div(lax.broadcasted_iota(i32, (rows // 8, rows), 1), i32(8))
        == lax.broadcasted_iota(i32, (rows // 8, rows), 0)
    )
    lo_rows[...] = dot(group, alone)
    sub8 = lax.broadcasted_iota(i32, (8, LANES), 0)
    piece = lax.div(lax.broadcasted_iota(i32, (8, LANES), 1), i32(links))
    first = piece == sub8
    second = piece + LANES // links == sub8
    low_id = lax.broadcasted_iota(i32, (LANES, 2 * LANES), 0).astype(f32)

    def count_group(g, carry):
        at = pl.ds(pl.multiple_of(8 * g, 8), 8)
        h8 = hi_tiled[at, :]
        key = jnp.concatenate([jnp.where(first, h8, -1.0), jnp.where(second, h8, -1.0)], axis=1)
        by_high = jnp.concatenate([jnp.where(key == float(v), 1.0, 0.0) for v in range(20)], axis=0).astype(bf16)
        by_low = flag(low_id == lo_rows[pl.ds(g, 1), :])
        found = dot_last(by_high, by_low)
        for v in range(20):
            counts[v // 2, at, (v % 2) * LANES : (v % 2 + 1) * LANES] = found[8 * v : 8 * v + 8, :]
        return carry

    with jax.named_scope("count"):
        lax.fori_loop(0, rows // 8, count_group, 0, unroll=4)

    def far_edges(i, carry):
        arrival = pltpu.make_async_remote_copy(
            src_ref=edges.at[i], dst_ref=edges.at[i], send_sem=es_sem.at[0], recv_sem=er_sem.at[i - 2],
            device_id={"patch": device[SIB]}, device_id_type=pl.DeviceIdType.MESH,
        )
        with jax.named_scope("wait_edges"):
            arrival.wait_recv()
        with jax.named_scope("use_edges"):
            use_edges(i)
        return carry

    with jax.named_scope("far_edges"):
        lax.fori_loop(2, 10, far_edges, 0)

    wait_for(upd_agg, upd_out, query_w, gain_ref)

    def node_copy(index, role, q):
        slot = NODE_SLOT[(MIRROR[role], q)]
        return remote(nodes.at[NODE_SLOT[(OWN, q)]], nodes.at[slot], ns_sem.at[index], nr_sem.at[slot - 4], role)

    head = rows // HEADS
    query_scale = math.log2(math.e) / math.sqrt(head)

    def unit(x, scale):
        parts = []
        for h in range(HEADS):
            part = x[:, h * head : (h + 1) * head]
            square = jnp.mean(part * part, axis=-1, keepdims=True)
            parts.append((part * (lax.rsqrt(square + HEAD_EPS) * scale)).astype(bf16))
        return jnp.concatenate(parts, axis=1)

    def rms_scale(x, gain):
        square = jnp.mean(x * x, axis=-1, keepdims=True)
        return (x * lax.rsqrt(square + NORM_EPS) * gain).astype(bf16)

    node_copies = []
    for c in range(2):
        with jax.named_scope("update"):
            at = slice(c * CHUNK, (c + 1) * CHUNK)
            update = silu(dot(summed[at, :].astype(bf16), upd_agg[...]) + base[at, :]).astype(bf16)
            latent = mesh_v[at, :].astype(f32) + dot(update, upd_out[...])
            encoded[at, :] = latent
            normed = rms_scale(latent, gain_ref[...])
            for q in (2 * c, 2 * c + 1):
                nodes[q] = normed[(q - 2 * c) * LANES : (q - 2 * c + 1) * LANES, :]
                node_copies += [node_copy(3 * q + index, role, q) for index, role in enumerate((NF, SIB, FW))]
                for copy in node_copies[-3:-1]:
                    copy.start()
    with jax.named_scope("queries"):
        for c in range(2):
            at = slice(c * CHUNK, (c + 1) * CHUNK)
            own = jnp.concatenate([nodes[2 * c], nodes[2 * c + 1]], axis=0)
            queries[at, :] = unit(dot(own, query_w[...]), query_scale)
    mixed[...] = jnp.zeros_like(mixed)
    values[...] = jnp.ones_like(values)
    wait_for(key_w, value_w)

    def pass_on(q):
        source, slot = NODE_SLOT[(FW, q)], NODE_SLOT[(OTH, q)]
        return remote(nodes.at[source], nodes.at[slot], ns_sem.at[12 + q], nr_sem.at[slot - 4], SIB)

    def arrived(slot):
        remote(nodes.at[slot], nodes.at[slot], ns_sem.at[0], nr_sem.at[slot - 4], SIB).wait_recv()

    def wait_nodes(i):
        for step_index in range(2, 10):
            @pl.when(i == step_index)
            def _():
                pair = NODE_USE[2 * step_index : 2 * step_index + 2]
                for role, q in sorted(pair, key=lambda block: block[0] != FW):
                    arrived(NODE_SLOT[(role, q)])
                    if role == FW:
                        pass_on(q).start()

    def attend(i, carry):
        for step_index in (1, 2):
            @pl.when(i == step_index)
            def _():
                for q in (2 * step_index - 2, 2 * step_index - 1):
                    node_copies[3 * q + 2].start()

        with jax.named_scope("wait_nodes"):
            wait_nodes(i)
        with jax.named_scope("attend_one"):
            attend_one(i)
        return carry

    def attend_one(i):
        features = jnp.concatenate([nodes[2 * i], nodes[2 * i + 1]], axis=0)
        keys = unit(dot(features, key_w[...]), 1.0)
        value = dot(features, value_w[...]).astype(bf16)
        for h in range(HEADS):
            values[:, 2 * h * head : (2 * h + 1) * head] = value[:, h * head : (h + 1) * head]
        for t in range(rows // CHUNK):
            at = slice(t * CHUNK, (t + 1) * CHUNK)
            often = counts[i, at, :]
            for h in range(HEADS):
                cols = slice(h * head, (h + 1) * head)
                score = dot_last(queries[at, cols], keys[:, cols])
                weight = (jnp.exp2(score) * often).astype(bf16)
                wide = slice(2 * h * head, 2 * (h + 1) * head)
                mixed[at, wide] += dot(weight, values[:, wide])

    with jax.named_scope("attend"):
        lax.fori_loop(0, 10, attend, 0)

    wait_for(out_w, ffn_in, ffn_out, ffn_gain_ref)

    with jax.named_scope("attended"):
        for t in range(rows // CHUNK):
            at = slice(t * CHUNK, (t + 1) * CHUNK)
            attended = jnp.concatenate(
                [
                    mixed[at, 2 * h * head : (2 * h + 1) * head] / mixed[at, (2 * h + 1) * head : 2 * (h + 1) * head]
                    for h in range(HEADS)
                ],
                axis=1,
            ).astype(bf16)
            hidden = encoded[at, :] + dot(attended, out_w[...])
            encoded[at, :] = hidden
            queries[at, :] = rms_scale(hidden, ffn_gain_ref[...])

    with jax.named_scope("expand"):
        for c in range(ffn_in.shape[1] // rows):
            cols = slice(rows * c, rows * (c + 1))
            expanded[:, cols] = silu(dot(queries[...], ffn_in[:, cols])).astype(bf16)

    with jax.named_scope("contract"):
        for t in range(rows // CHUNK):
            at = slice(t * CHUNK, (t + 1) * CHUNK)
            result_ref[at, :] = (encoded[at, :] + dot(expanded[at, :], ffn_out[...])).astype(bf16)

    for copy in land_copies + [edge_copy(k) for k in range(8)] + node_copies + [pass_on(q) for q in range(4)]:
        copy.wait_send()


def shards(
    grid_latents, mesh_latents, enc_send, enc_recv, neighbours,
    enc_grid_w, enc_bias, enc_mesh_w, enc_msg_w, upd_agg_w, upd_mesh_w, upd_out_w,
    norm_gain, query_w, key_w, value_w, out_w, ffn_gain, ffn_in_w, ffn_out_w,
):
    count = lax.axis_size("patch")
    rows, width = mesh_latents.shape
    hbm_spec = pl.BlockSpec(memory_space=pltpu.HBM)
    vmem_spec = pl.BlockSpec(memory_space=pltpu.VMEM)
    square = pltpu.VMEM((width, width), bf16)
    args = (
        grid_latents, mesh_latents, enc_send, enc_recv, neighbours.T,
        enc_grid_w, enc_bias[None, :], enc_mesh_w, enc_msg_w, upd_agg_w, upd_mesh_w, upd_out_w,
        norm_gain[None, :], query_w, key_w, value_w, out_w, ffn_gain[None, :], ffn_in_w, ffn_out_w,
    )
    return pl.pallas_call(
        functools.partial(kernel, count),
        out_shape=pltpu.VMEM((rows, width), bf16),
        in_specs=[hbm_spec] * len(args),
        out_specs=vmem_spec,
        scratch_shapes=[
            pltpu.VMEM(grid_latents.shape, bf16),
            pltpu.VMEM((rows, width), bf16),
            pltpu.VMEM(enc_send.shape, i32),
            pltpu.VMEM(enc_recv.shape, i32),
            pltpu.VMEM(neighbours.shape[::-1], i32),
            *([pltpu.VMEM((1, width), f32)] * 3),
            *([square] * 10),
            pltpu.VMEM(ffn_in_w.shape, bf16),
            pltpu.VMEM(ffn_out_w.shape, bf16),
            pltpu.VMEM(grid_latents.shape, bf16),
            pltpu.VMEM((rows, width), bf16),
            pltpu.VMEM((10, CHUNK, width), bf16),
            pltpu.VMEM((rows, width), f32),
            pltpu.VMEM((rows, width), f32),
            pltpu.VMEM((rows, width), f32),
            pltpu.VMEM((18, CHUNK, width), bf16),
            pltpu.VMEM((20, LANES, width), bf16),
            pltpu.VMEM((10, rows, CHUNK), f32),
            pltpu.VMEM((rows, width), bf16),
            pltpu.VMEM((CHUNK, 2 * width), bf16),
            pltpu.VMEM((rows, 2 * width), f32),
            pltpu.VMEM((20, LANES, LANES), i32),
            pltpu.VMEM((20, LANES, LANES), i32),
            pltpu.VMEM((20, 1, LANES), i32),
            pltpu.VMEM((LANES, LANES), i32),
            pltpu.VMEM((5, 8, LANES), i32),
            pltpu.VMEM((5, 8, LANES), i32),
            pltpu.VMEM((rows, LANES), f32),
            pltpu.VMEM((rows // 8, 2 * LANES), f32),
            pltpu.VMEM((rows, ffn_in_w.shape[1]), bf16),
            pltpu.SemaphoreType.DMA((20,)),
            pltpu.SemaphoreType.DMA((4,)),
            pltpu.SemaphoreType.DMA((4,)),
            pltpu.SemaphoreType.DMA((8,)),
            pltpu.SemaphoreType.DMA((8,)),
            pltpu.SemaphoreType.DMA((16,)),
            pltpu.SemaphoreType.DMA((16,)),
        ],
        compiler_params=pltpu.CompilerParams(
            collective_id=0, has_side_effects=True, vmem_limit_bytes=62 * 2**20
        ),
        name="encode_attend",
    )(*args)


def solution(mesh):
    split = P(("groups", "patch"), None)
    in_specs = (split,) * 5 + (P(),) * 15
    return jax.shard_map(shards, mesh=mesh, in_specs=in_specs, out_specs=split, check_vma=False)
```

time: 75.5 us -> 63.8 us (0.85)
  Pallas kernels: 71.8 us -> 62.9 us
  local copies, waits for them, and re-layouts: 3.54 us -> 0.8 us
    pallas_call x1, Pallas kernels: 71.8 us -> 62.9 us  [shards(): pl.pallas_call(functools.partial(kernel, count), out_shape=pltpu.VMEM((ro...]
    unnamed x2 -> x1, local copies, waits for them, and re-layouts: 3.54 us -> 0.8 us
where the time goes in v1:
time: 63.8 us; the launch traced here: 63.7 us
  Pallas kernels  62.9 us (99%)
  local copies, waits for them, and re-layouts  0.8 us (1%)
    pallas_call x1, Pallas kernels, shards(): pl.pallas_call(functools.partial(kernel, count), out_shape=pltpu.VMEM((ro...  62.9 us

profile of v1, /device:TPU:513, one launch (start us, length us, event | category | flops | bytes accessed | tf_op | source)
XLA Modules:
  0.0 63.7 jit_solution(2388034707363168103)
XLA Ops:
  0.0 62.9 %encode_attend.1 = bf16[512,512]{1,0:T(8,128)(2,1)S(1)} custom-call(bf16[1024,512]{1,0:T(8,128)(2,1)} %grid_hbm.1, bf16[512,512]{1,0:T(8,128)(2,1)} %mesh_hbm.1, s32[20,128]{1,0:T(8,128)} %send_hbm.1, s32[20,128]{1,0:T(8,128)} %recv_hbm.1, s32[32,512]{1,0:T(8,128)} %bitcast.4, bf16[512,512]{1,0:T(8,128)(2,1)} %grid_w_hbm.1, f32[1,512]{1,0:T(1,128)} %bitcast.5, ...), custom_call_target="tpu_custom_call" | custom-call | tf_op jit(solution)/shard_map/encode_attend/pallas_call | solution.py:416
  62.9 0.8 %copy.22 = bf16[512,512]{1,0:T(8,128)(2,1)} copy(bf16[512,512]{1,0:T(8,128)(2,1)S(1)} %encode_attend.1) | data formatting | bytes 1048576

commit v2 on v1

--- a/solution.py
+++ b/solution.py
@@ -25,8 +25,8 @@
 EDGE_SLOT = {key: slot for slot, key in enumerate(EDGE_USE)}
 NODE_USE = (
     [(OWN, q) for q in range(4)] + [(SIB, q) for q in range(4)]
-    + [(FW, 0), (FW, 1), (OTH, 0), (OTH, 1), (FW, 2), (NF, 0)]
-    + [(FW, 3), (OTH, 2), (OTH, 3), (NF, 1), (NF, 2), (NF, 3)]
+    + [(FW, 0), (FW, 1), (OTH, 0), (OTH, 1), (FW, 2), (FW, 3), (OTH, 2), (OTH, 3)]
+    + [(NF, q) for q in range(4)]
 )
 NODE_SLOT = {key: slot for slot, key in enumerate(NODE_USE)}
 
@@ -121,10 +121,10 @@
     for b in range(20):
         send_cols[b] = jnp.broadcast_to(turned[:, b : b + 1], (LANES, LANES))
 
-    lane = lax.broadcasted_iota(i32, (CHUNK, LANES), 1)
+    lane = lax.broadcasted_iota(i32, (4 * LANES, LANES), 1)
 
     def onehot(cols, k, width):
-        col = jnp.concatenate([cols[2 * k], cols[2 * k + 1]], axis=0)
+        col = jnp.concatenate([cols[4 * k + j] for j in range(4)], axis=0)
         return jnp.concatenate([flag(col == lane + LANES * t) for t in range(width // LANES)], axis=1)
 
     with jax.named_scope("wait_grid"):
@@ -146,7 +146,9 @@
 
     def pick(k, carry):
         chosen = onehot(send_cols, k, grid_v.shape[0])
-        edges[(10 + k) % 18] = dot(chosen, projected[...]).astype(bf16)
+        picked = dot(chosen, projected[...]).astype(bf16)
+        for c in range(2):
+            edges[(10 + 2 * k + c) % 18] = picked[c * CHUNK : (c + 1) * CHUNK, :]
 
         @pl.when(k == 0)
         def _():
@@ -154,14 +156,15 @@
             for copy in land_copies:
                 copy.start()
 
-        for index in range(8):
+        for index in range(4):
             @pl.when(k == index)
             def _():
-                edge_copy(index).start()
+                edge_copy(2 * index).start()
+                edge_copy(2 * index + 1).start()
         return carry
 
     with jax.named_scope("pick"):
-        lax.fori_loop(0, 10, pick, 0)
+        lax.fori_loop(0, 5, pick, 0)
 
     wait_for(mesh_v, mesh_w, upd_mesh)
 
@@ -190,24 +193,28 @@
     wait_for(msg_w)
 
     def receive(i, carry):
-        received[i] = dot(onehot(land_cols, i, rows), receiver[...]).astype(bf16)
+        picked = dot(onehot(land_cols, i, rows), receiver[...]).astype(bf16)
+        for c in range(2):
+            received[2 * i + c] = picked[c * CHUNK : (c + 1) * CHUNK, :]
         return carry
 
     def use_edges(i):
-        active = silu(edges[i].astype(f32) + received[i].astype(f32)).astype(bf16)
-        message = dot(active, msg_w[...]).astype(bf16)
-        landing = jnp.concatenate([land_rows[2 * i], land_rows[2 * i + 1]], axis=1)
-        scatter = flag(lax.broadcasted_iota(i32, (rows, CHUNK), 0) == landing)
-        summed[...] += dot(scatter, message)
+        messages = []
+        for c in range(2):
+            active = silu(edges[2 * i + c].astype(f32) + received[2 * i + c].astype(f32)).astype(bf16)
+            messages.append(dot(active, msg_w[...]).astype(bf16))
+        landing = jnp.concatenate([land_rows[4 * i + j] for j in range(4)], axis=1)
+        scatter = flag(lax.broadcasted_iota(i32, (rows, 2 * CHUNK), 0) == landing)
+        summed[...] += dot(scatter, jnp.concatenate(messages, axis=0))
 
     def own_edges(i, carry):
         use_edges(i)
         return carry
 
     with jax.named_scope("receive"):
-        lax.fori_loop(0, 10, receive, 0)
+        lax.fori_loop(0, 5, receive, 0)
     with jax.named_scope("own_edges"):
-        lax.fori_loop(0, 2, own_edges, 0)
+        lax.fori_loop(0, 1, own_edges, 0)
 
     wait_for(neigh_ref)
     neigh = neigh_ref[...]
@@ -256,25 +263,24 @@
         by_low = flag(low_id == lo_rows[pl.ds(g, 1), :])
         found = dot_last(by_high, by_low)
         for v in range(20):
-            counts[v // 2, at, (v % 2) * LANES : (v % 2 + 1) * LANES] = found[8 * v : 8 * v + 8, :]
+            counts[v // 4, at, (v % 4) * LANES : (v % 4 + 1) * LANES] = found[8 * v : 8 * v + 8, :]
         return carry
 
     with jax.named_scope("count"):
-        lax.fori_loop(0, rows // 8, count_group, 0, unroll=4)
+        lax.fori_loop(0, rows // 8, count_group, 0, unroll=8)
 
     def far_edges(i, carry):
-        arrival = pltpu.make_async_remote_copy(
-            src_ref=edges.at[i], dst_ref=edges.at[i], send_sem=es_sem.at[0], recv_sem=er_sem.at[i - 2],
-            device_id={"patch": device[SIB]}, device_id_type=pl.DeviceIdType.MESH,
-        )
         with jax.named_scope("wait_edges"):
-            arrival.wait_recv()
+            for c in range(2):
+                remote(
+                    edges.at[2 * i + c], edges.at[2 * i + c], es_sem.at[0], er_sem.at[2 * i + c - 2], SIB
+                ).wait_recv()
         with jax.named_scope("use_edges"):
             use_edges(i)
         return carry
 
     with jax.named_scope("far_edges"):
-        lax.fori_loop(2, 10, far_edges, 0)
+        lax.fori_loop(1, 5, far_edges, 0)
 
     wait_for(upd_agg, upd_out, query_w, gain_ref)
 
@@ -327,21 +333,19 @@
         remote(nodes.at[slot], nodes.at[slot], ns_sem.at[0], nr_sem.at[slot - 4], SIB).wait_recv()
 
     def wait_nodes(i):
-        for step_index in range(2, 10):
+        for step_index in range(1, 5):
             @pl.when(i == step_index)
             def _():
-                pair = NODE_USE[2 * step_index : 2 * step_index + 2]
-                for role, q in sorted(pair, key=lambda block: block[0] != FW):
+                for role, q in NODE_USE[4 * step_index : 4 * step_index + 4]:
                     arrived(NODE_SLOT[(role, q)])
                     if role == FW:
                         pass_on(q).start()
 
     def attend(i, carry):
-        for step_index in (1, 2):
-            @pl.when(i == step_index)
-            def _():
-                for q in (2 * step_index - 2, 2 * step_index - 1):
-                    node_copies[3 * q + 2].start()
+        @pl.when(i == 1)
+        def _():
+            for q in range(4):
+                node_copies[3 * q + 2].start()
 
         with jax.named_scope("wait_nodes"):
             wait_nodes(i)
@@ -350,7 +354,7 @@
         return carry
 
     def attend_one(i):
-        features = jnp.concatenate([nodes[2 * i], nodes[2 * i + 1]], axis=0)
+        features = jnp.concatenate([nodes[4 * i + j] for j in range(4)], axis=0)
         keys = unit(dot(features, key_w[...]), 1.0)
         value = dot(features, value_w[...]).astype(bf16)
         for h in range(HEADS):
@@ -366,7 +370,7 @@
                 mixed[at, wide] += dot(weight, values[:, wide])
 
     with jax.named_scope("attend"):
-        lax.fori_loop(0, 10, attend, 0)
+        lax.fori_loop(0, 5, attend, 0)
 
     wait_for(out_w, ffn_in, ffn_out, ffn_gain_ref)
 
@@ -436,9 +440,9 @@
             pltpu.VMEM((rows, width), f32),
             pltpu.VMEM((18, CHUNK, width), bf16),
             pltpu.VMEM((20, LANES, width), bf16),
-            pltpu.VMEM((10, rows, CHUNK), f32),
+            pltpu.VMEM((5, rows, 4 * LANES), f32),
             pltpu.VMEM((rows, width), bf16),
-            pltpu.VMEM((CHUNK, 2 * width), bf16),
+            pltpu.VMEM((4 * LANES, 2 * width), bf16),
             pltpu.VMEM((rows, 2 * width), f32),
             pltpu.VMEM((20, LANES, LANES), i32),
             pltpu.VMEM((20, LANES, LANES), i32),

time: 63.8 us -> 65.1 us (1.020)
  Pallas kernels: 62.9 us -> 64.2 us
    pallas_call x1, Pallas kernels: 62.9 us -> 64.2 us  [shards(): pl.pallas_call(functools.partial(kernel, count), out_shape=pltpu.VMEM((ro...]
where the time goes in v2:
time: 65.1 us; the launch traced here: 65 us
  Pallas kernels  64.2 us (99%)
  local copies, waits for them, and re-layouts  0.8 us (1%)
    pallas_call x1, Pallas kernels, shards(): pl.pallas_call(functools.partial(kernel, count), out_shape=pltpu.VMEM((ro...  64.2 us

profile of v2, /device:TPU:513, one launch (start us, length us, event | category | flops | bytes accessed | tf_op | source)
XLA Modules:
  0.0 65.0 jit_solution(12707926787420833418)
XLA Ops:
  0.0 64.2 %encode_attend.1 = bf16[512,512]{1,0:T(8,128)(2,1)S(1)} custom-call(bf16[1024,512]{1,0:T(8,128)(2,1)} %grid_hbm.1, bf16[512,512]{1,0:T(8,128)(2,1)} %mesh_hbm.1, s32[20,128]{1,0:T(8,128)} %send_hbm.1, s32[20,128]{1,0:T(8,128)} %recv_hbm.1, s32[32,512]{1,0:T(8,128)} %bitcast.4, bf16[512,512]{1,0:T(8,128)(2,1)} %grid_w_hbm.1, f32[1,512]{1,0:T(1,128)} %bitcast.5, ...), custom_call_target="tpu_custom_call" | custom-call | tf_op jit(solution)/shard_map/encode_attend/pallas_call | solution.py:420
  64.2 0.8 %copy.22 = bf16[512,512]{1,0:T(8,128)(2,1)} copy(bf16[512,512]{1,0:T(8,128)(2,1)S(1)} %encode_attend.1) | data formatting | bytes 1048576

commit v3 on v2

--- a/solution.py
+++ b/solution.py
@@ -25,8 +25,8 @@
 EDGE_SLOT = {key: slot for slot, key in enumerate(EDGE_USE)}
 NODE_USE = (
     [(OWN, q) for q in range(4)] + [(SIB, q) for q in range(4)]
-    + [(FW, 0), (FW, 1), (OTH, 0), (OTH, 1), (FW, 2), (FW, 3), (OTH, 2), (OTH, 3)]
-    + [(NF, q) for q in range(4)]
+    + [(FW, 0), (FW, 1), (OTH, 0), (OTH, 1), (FW, 2), (NF, 0)]
+    + [(OTH, 2), (NF, 1), (FW, 3), (NF, 2), (OTH, 3), (NF, 3)]
 )
 NODE_SLOT = {key: slot for slot, key in enumerate(NODE_USE)}
 
@@ -65,7 +65,7 @@
     grid_v, mesh_v, send_ref, recv_ref, neigh_ref, bias_ref, gain_ref, ffn_gain_ref, grid_w, mesh_w, msg_w, upd_agg, upd_mesh, upd_out, query_w, key_w, value_w, out_w, ffn_in, ffn_out,
     projected, receiver, received, base, summed, encoded, edges, nodes, counts, queries, values, mixed,
     send_cols, land_cols, land_rows, stage, land_send, land_recv, hi_tiled, lo_rows, expanded,
-    load_sem, ls_sem, lr_sem, es_sem, er_sem, ns_sem, nr_sem,
+    load_sem, ls_sem, lr_sem, es_sem, er_sem, ns_sem, nr_sem, relay_send, relay_recv,
 ):
     me = lax.axis_index("patch")
     sign = 1 - 2 * (me % 2)
@@ -96,7 +96,7 @@
             loads[id(ref)].wait()
 
     barrier = pltpu.get_barrier_semaphore()
-    for role in (SIB, OTH, FW, NF):
+    for role in (SIB, FW, NF):
         pl.semaphore_signal(
             barrier, inc=1, device_id={"patch": device[role]}, device_id_type=pl.DeviceIdType.MESH
         )
@@ -114,8 +114,10 @@
 
     land_copies = [
         remote(land_send.at[role], land_recv.at[MIRROR[role]], ls_sem.at[role - 1], lr_sem.at[MIRROR[role] - 1], role)
-        for role in (SIB, OTH, FW, NF)
+        for role in (SIB, FW, NF)
     ]
+    land_copies.append(remote(land_send.at[OTH], land_recv.at[OWN], ls_sem.at[OTH - 1], relay_recv.at[2], SIB))
+    land_relay = remote(land_recv.at[OWN], land_recv.at[OTH], relay_send.at[2], lr_sem.at[OTH - 1], FW)
 
     turned = stage[...].T
     for b in range(20):
@@ -133,16 +135,45 @@
 
     def project(t, carry):
         at = pl.ds(pl.multiple_of(t * rows, rows), rows)
-        projected[at, :] = (dot(grid_v[at, :], grid_w[...]) + bias_ref[...]).astype(bf16)
-        return carry
+        projected[at, :] = project_rows(grid_v[at, :])
+        return carry
+
+    def edge_copy(k):
+        role, half = EDGE_SEND[k]
+        if role == OTH:
+            return remote(edges.at[10 + k], edges.at[18 + half], es_sem.at[k], relay_recv.at[half], SIB)
+        slot = EDGE_SLOT[(MIRROR[role], half)]
+        return remote(edges.at[10 + k], edges.at[slot], es_sem.at[k], er_sem.at[slot - 2], role)
+
+    def edge_relay(half):
+        slot = EDGE_SLOT[(OTH, half)]
+        return remote(edges.at[18 + half], edges.at[slot], relay_send.at[half], er_sem.at[slot - 2], FW)
+
+    def relay_arrived(index, buffer):
+        remote(buffer, buffer, es_sem.at[0], relay_recv.at[index], SIB).wait_recv()
+
+    def pick_first():
+        picked = dot(onehot(send_cols, 0, grid_v.shape[0]), grid_v[...]).astype(bf16)
+        for c in range(2):
+            edges[10 + c] = picked[c * CHUNK : (c + 1) * CHUNK, :]
+
+    with jax.named_scope("pick_first"):
+        pick_first()
+        pl.semaphore_wait(barrier, 3)
+        for copy in land_copies:
+            copy.start()
+        for k in range(2):
+            edge_copy(k).start()
+
+    def project_rows(values):
+        return (dot(values, grid_w[...]) + bias_ref[...]).astype(bf16)
 
     with jax.named_scope("project"):
         lax.fori_loop(0, grid_v.shape[0] // rows, project, 0)
 
-    def edge_copy(k):
-        role, half = EDGE_SEND[k]
-        slot = EDGE_SLOT[(MIRROR[role], half)]
-        return remote(edges.at[10 + k], edges.at[slot], es_sem.at[k], er_sem.at[slot - 2], role)
+    with jax.named_scope("relay_rows"):
+        relay_arrived(2, land_recv.at[OWN])
+        land_relay.start()
 
     def pick(k, carry):
         chosen = onehot(send_cols, k, grid_v.shape[0])
@@ -150,13 +181,7 @@
         for c in range(2):
             edges[(10 + 2 * k + c) % 18] = picked[c * CHUNK : (c + 1) * CHUNK, :]
 
-        @pl.when(k == 0)
-        def _():
-            pl.semaphore_wait(barrier, 4)
-            for copy in land_copies:
-                copy.start()
-
-        for index in range(4):
+        for index in range(1, 4):
             @pl.when(k == index)
             def _():
                 edge_copy(2 * index).start()
@@ -164,7 +189,12 @@
         return carry
 
     with jax.named_scope("pick"):
-        lax.fori_loop(0, 5, pick, 0)
+        lax.fori_loop(1, 5, pick, 0)
+
+    with jax.named_scope("relay_edges"):
+        for half in range(2):
+            relay_arrived(half, edges.at[18 + half])
+            edge_relay(half).start()
 
     wait_for(mesh_v, mesh_w, upd_mesh)
 
@@ -179,17 +209,24 @@
     with jax.named_scope("prepare"):
         lax.fori_loop(0, rows // CHUNK, prepare, 0)
 
-    for role in (SIB, OTH, FW, NF):
-        remote(land_send.at[role], land_recv.at[role], ls_sem.at[role - 1], lr_sem.at[role - 1], role).wait_recv()
-    for i, (role, half) in enumerate(EDGE_USE):
-        source = land_send if role == OWN else land_recv
-        for j in range(2):
-            row = source[role, 2 * half + j : 2 * half + j + 1, :]
-            land_rows[2 * i + j] = row
-            stage[2 * i + j : 2 * i + j + 1, :] = row
-    landed = stage[...].T
-    for b in range(20):
-        land_cols[b] = jnp.broadcast_to(landed[:, b : b + 1], (LANES, LANES))
+    def place_receivers(pairs):
+        for i in pairs:
+            role, half = EDGE_USE[i]
+            if role != OWN and half == 0:
+                remote(
+                    land_send.at[role], land_recv.at[role], ls_sem.at[role - 1], lr_sem.at[role - 1], role
+                ).wait_recv()
+            source = land_send if role == OWN else land_recv
+            for j in range(2):
+                row = source[role, 2 * half + j : 2 * half + j + 1, :]
+                land_rows[2 * i + j] = row
+                stage[2 * i + j : 2 * i + j + 1, :] = row
+        landed = stage[...].T
+        for i in pairs:
+            for b in (2 * i, 2 * i + 1):
+                land_cols[b] = jnp.broadcast_to(landed[:, b : b + 1], (LANES, LANES))
+
+    place_receivers(range(8))
     wait_for(msg_w)
 
     def receive(i, carry):
@@ -212,7 +249,7 @@
         return carry
 
     with jax.named_scope("receive"):
-        lax.fori_loop(0, 5, receive, 0)
+        lax.fori_loop(0, 4, receive, 0)
     with jax.named_scope("own_edges"):
         lax.fori_loop(0, 1, own_edges, 0)
 
@@ -263,7 +300,7 @@
         by_low = flag(low_id == lo_rows[pl.ds(g, 1), :])
         found = dot_last(by_high, by_low)
         for v in range(20):
-            counts[v // 4, at, (v % 4) * LANES : (v % 4 + 1) * LANES] = found[8 * v : 8 * v + 8, :]
+            counts[v // 2, at, (v % 2) * LANES : (v % 2 + 1) * LANES] = found[8 * v : 8 * v + 8, :]
         return carry
 
     with jax.named_scope("count"):
@@ -275,10 +312,18 @@
                 remote(
                     edges.at[2 * i + c], edges.at[2 * i + c], es_sem.at[0], er_sem.at[2 * i + c - 2], SIB
                 ).wait_recv()
+        @pl.when(i == 2)
+        def _():
+            for c in range(2):
+                edges[4 + c] = project_rows(edges[4 + c])
+
         with jax.named_scope("use_edges"):
             use_edges(i)
         return carry
 
+    with jax.named_scope("receive_last"):
+        place_receivers((8, 9))
+        receive(4, 0)
     with jax.named_scope("far_edges"):
         lax.fori_loop(1, 5, far_edges, 0)
 
@@ -332,45 +377,56 @@
     def arrived(slot):
         remote(nodes.at[slot], nodes.at[slot], ns_sem.at[0], nr_sem.at[slot - 4], SIB).wait_recv()
 
-    def wait_nodes(i):
-        for step_index in range(1, 5):
-            @pl.when(i == step_index)
-            def _():
-                for role, q in NODE_USE[4 * step_index : 4 * step_index + 4]:
-                    arrived(NODE_SLOT[(role, q)])
-                    if role == FW:
-                        pass_on(q).start()
-
-    def attend(i, carry):
-        @pl.when(i == 1)
-        def _():
-            for q in range(4):
-                node_copies[3 * q + 2].start()
-
-        with jax.named_scope("wait_nodes"):
-            wait_nodes(i)
-        with jax.named_scope("attend_one"):
-            attend_one(i)
-        return carry
-
-    def attend_one(i):
-        features = jnp.concatenate([nodes[4 * i + j] for j in range(4)], axis=0)
+    def wait_nodes(blocks):
+        for role, q in blocks:
+            arrived(NODE_SLOT[(role, q)])
+            if role == FW:
+                pass_on(q).start()
+
+    def attend(block, pairs):
+        size = 2 * pairs * LANES
+        features = jnp.concatenate([nodes[block + j] for j in range(2 * pairs)], axis=0)
         keys = unit(dot(features, key_w[...]), 1.0)
         value = dot(features, value_w[...]).astype(bf16)
         for h in range(HEADS):
-            values[:, 2 * h * head : (2 * h + 1) * head] = value[:, h * head : (h + 1) * head]
+            values[:size, 2 * h * head : (2 * h + 1) * head] = value[:, h * head : (h + 1) * head]
         for t in range(rows // CHUNK):
             at = slice(t * CHUNK, (t + 1) * CHUNK)
-            often = counts[i, at, :]
+            often = jnp.concatenate([counts[block // 2 + j, at, :] for j in range(pairs)], axis=1)
             for h in range(HEADS):
                 cols = slice(h * head, (h + 1) * head)
                 score = dot_last(queries[at, cols], keys[:, cols])
                 weight = (jnp.exp2(score) * often).astype(bf16)
                 wide = slice(2 * h * head, 2 * (h + 1) * head)
-                mixed[at, wide] += dot(weight, values[:, wide])
-
+                mixed[at, wide] += dot(weight, values[:size, wide])
+
+    def attend_chip(i, carry):
+        @pl.when(i == 1)
+        def _():
+            with jax.named_scope("wait_sib"):
+                wait_nodes(NODE_USE[4:8])
+
+        with jax.named_scope("attend_four"):
+            attend(4 * i, 2)
+        return carry
+
+    def attend_far(i, carry):
+        with jax.named_scope("wait_nodes"):
+            for index in range(6):
+                @pl.when(i == index)
+                def _():
+                    wait_nodes(NODE_USE[8 + 2 * index : 10 + 2 * index])
+
+        with jax.named_scope("attend_two"):
+            attend(8 + 2 * i, 1)
+        return carry
+
+    with jax.named_scope("attend_chip"):
+        lax.fori_loop(0, 2, attend_chip, 0)
+    for q in range(4):
+        node_copies[3 * q + 2].start()
     with jax.named_scope("attend"):
-        lax.fori_loop(0, 5, attend, 0)
+        lax.fori_loop(0, 6, attend_far, 0)
 
     wait_for(out_w, ffn_in, ffn_out, ffn_gain_ref)
 
@@ -398,7 +454,7 @@
             at = slice(t * CHUNK, (t + 1) * CHUNK)
             result_ref[at, :] = (encoded[at, :] + dot(expanded[at, :], ffn_out[...])).astype(bf16)
 
-    for copy in land_copies + [edge_copy(k) for k in range(8)] + node_copies + [pass_on(q) for q in range(4)]:
+    for copy in land_copies + [edge_copy(k) for k in range(8)] + node_copies + [pass_on(q) for q in range(4)] + [land_relay, edge_relay(0), edge_relay(1)]:
         copy.wait_send()
 
 
@@ -438,9 +494,9 @@
             pltpu.VMEM((rows, width), f32),
             pltpu.VMEM((rows, width), f32),
             pltpu.VMEM((rows, width), f32),
-            pltpu.VMEM((18, CHUNK, width), bf16),
+            pltpu.VMEM((20, CHUNK, width), bf16),
             pltpu.VMEM((20, LANES, width), bf16),
-            pltpu.VMEM((5, rows, 4 * LANES), f32),
+            pltpu.VMEM((10, rows, 2 * LANES), f32),
             pltpu.VMEM((rows, width), bf16),
             pltpu.VMEM((4 * LANES, 2 * width), bf16),
             pltpu.VMEM((rows, 2 * width), f32),
@@ -460,6 +516,8 @@
             pltpu.SemaphoreType.DMA((8,)),
             pltpu.SemaphoreType.DMA((16,)),
             pltpu.SemaphoreType.DMA((16,)),
+            pltpu.SemaphoreType.DMA((3,)),
+            pltpu.SemaphoreType.DMA((3,)),
         ],
         compiler_params=pltpu.CompilerParams(
             collective_id=0, has_side_effects=True, vmem_limit_bytes=62 * 2**20

time: 65.1 us -> 62.6 us (0.962)
  Pallas kernels: 64.2 us -> 61.7 us
    pallas_call x1, Pallas kernels: 64.2 us -> 61.7 us  [shards(): pl.pallas_call(functools.partial(kernel, count), out_shape=pltpu.VMEM((ro...]
where the time goes in v3:
time: 62.6 us; the launch traced here: 62.5 us
  Pallas kernels  61.7 us (99%)
  local copies, waits for them, and re-layouts  0.8 us (1%)
    pallas_call x1, Pallas kernels, shards(): pl.pallas_call(functools.partial(kernel, count), out_shape=pltpu.VMEM((ro...  61.7 us

profile of v3, /device:TPU:513, one launch (start us, length us, event | category | flops | bytes accessed | tf_op | source)
XLA Modules:
  0.0 62.5 jit_solution(266673564955290077)
XLA Ops:
  0.0 61.7 %encode_attend.1 = bf16[512,512]{1,0:T(8,128)(2,1)S(1)} custom-call(bf16[1024,512]{1,0:T(8,128)(2,1)} %grid_hbm.1, bf16[512,512]{1,0:T(8,128)(2,1)} %mesh_hbm.1, s32[20,128]{1,0:T(8,128)} %send_hbm.1, s32[20,128]{1,0:T(8,128)} %recv_hbm.1, s32[32,512]{1,0:T(8,128)} %bitcast.4, bf16[512,512]{1,0:T(8,128)(2,1)} %grid_w_hbm.1, f32[1,512]{1,0:T(1,128)} %bitcast.5, ...), custom_call_target="tpu_custom_call" | custom-call | tf_op jit(solution)/shard_map/encode_attend/pallas_call | solution.py:476
  61.7 0.8 %copy.22 = bf16[512,512]{1,0:T(8,128)(2,1)} copy(bf16[512,512]{1,0:T(8,128)(2,1)S(1)} %encode_attend.1) | data formatting | bytes 1048576

commit v4 on v3

--- a/solution.py
+++ b/solution.py
@@ -171,10 +171,6 @@
     with jax.named_scope("project"):
         lax.fori_loop(0, grid_v.shape[0] // rows, project, 0)
 
-    with jax.named_scope("relay_rows"):
-        relay_arrived(2, land_recv.at[OWN])
-        land_relay.start()
-
     def pick(k, carry):
         chosen = onehot(send_cols, k, grid_v.shape[0])
         picked = dot(chosen, projected[...]).astype(bf16)
@@ -190,11 +186,6 @@
 
     with jax.named_scope("pick"):
         lax.fori_loop(1, 5, pick, 0)
-
-    with jax.named_scope("relay_edges"):
-        for half in range(2):
-            relay_arrived(half, edges.at[18 + half])
-            edge_relay(half).start()
 
     wait_for(mesh_v, mesh_w, upd_mesh)
 
@@ -208,50 +199,6 @@
 
     with jax.named_scope("prepare"):
         lax.fori_loop(0, rows // CHUNK, prepare, 0)
-
-    def place_receivers(pairs):
-        for i in pairs:
-            role, half = EDGE_USE[i]
-            if role != OWN and half == 0:
-                remote(
-                    land_send.at[role], land_recv.at[role], ls_sem.at[role - 1], lr_sem.at[role - 1], role
-                ).wait_recv()
-            source = land_send if role == OWN else land_recv
-            for j in range(2):
-                row = source[role, 2 * half + j : 2 * half + j + 1, :]
-                land_rows[2 * i + j] = row
-                stage[2 * i + j : 2 * i + j + 1, :] = row
-        landed = stage[...].T
-        for i in pairs:
-            for b in (2 * i, 2 * i + 1):
-                land_cols[b] = jnp.broadcast_to(landed[:, b : b + 1], (LANES, LANES))
-
-    place_receivers(range(8))
-    wait_for(msg_w)
-
-    def receive(i, carry):
-        picked = dot(onehot(land_cols, i, rows), receiver[...]).astype(bf16)
-        for c in range(2):
-            received[2 * i + c] = picked[c * CHUNK : (c + 1) * CHUNK, :]
-        return carry
-
-    def use_edges(i):
-        messages = []
-        for c in range(2):
-            active = silu(edges[2 * i + c].astype(f32) + received[2 * i + c].astype(f32)).astype(bf16)
-            messages.append(dot(active, msg_w[...]).astype(bf16))
-        landing = jnp.concatenate([land_rows[4 * i + j] for j in range(4)], axis=1)
-        scatter = flag(lax.broadcasted_iota(i32, (rows, 2 * CHUNK), 0) == landing)
-        summed[...] += dot(scatter, jnp.concatenate(messages, axis=0))
-
-    def own_edges(i, carry):
-        use_edges(i)
-        return carry
-
-    with jax.named_scope("receive"):
-        lax.fori_loop(0, 4, receive, 0)
-    with jax.named_scope("own_edges"):
-        lax.fori_loop(0, 1, own_edges, 0)
 
     wait_for(neigh_ref)
     neigh = neigh_ref[...]
@@ -305,6 +252,59 @@
 
     with jax.named_scope("count"):
         lax.fori_loop(0, rows // 8, count_group, 0, unroll=8)
+
+    with jax.named_scope("relay_rows"):
+        relay_arrived(2, land_recv.at[OWN])
+        land_relay.start()
+
+    with jax.named_scope("relay_edges"):
+        for half in range(2):
+            relay_arrived(half, edges.at[18 + half])
+            edge_relay(half).start()
+
+    def place_receivers(pairs):
+        for i in pairs:
+            role, half = EDGE_USE[i]
+            if role != OWN and half == 0:
+                remote(
+                    land_send.at[role], land_recv.at[role], ls_sem.at[role - 1], lr_sem.at[role - 1], role
+                ).wait_recv()
+            source = land_send if role == OWN else land_recv
+            for j in range(2):
+                row = source[role, 2 * half + j : 2 * half + j + 1, :]
+                land_rows[2 * i + j] = row
+                stage[2 * i + j : 2 * i + j + 1, :] = row
+        landed = stage[...].T
+        for i in pairs:
+            for b in (2 * i, 2 * i + 1):
+                land_cols[b] = jnp.broadcast_to(landed[:, b : b + 1], (LANES, LANES))
+
+    place_receivers(range(8))
+    wait_for(msg_w)
+
+    def receive(i, carry):
+        picked = dot(onehot(land_cols, i, rows), receiver[...]).astype(bf16)
+        for c in range(2):
+            received[2 * i + c] = picked[c * CHUNK : (c + 1) * CHUNK, :]
+        return carry
+
+    def use_edges(i):
+        messages = []
+        for c in range(2):
+            active = silu(edges[2 * i + c].astype(f32) + received[2 * i + c].astype(f32)).astype(bf16)
+            messages.append(dot(active, msg_w[...]).astype(bf16))
+        landing = jnp.concatenate([land_rows[4 * i + j] for j in range(4)], axis=1)
+        scatter = flag(lax.broadcasted_iota(i32, (rows, 2 * CHUNK), 0) == landing)
+        summed[...] += dot(scatter, jnp.concatenate(messages, axis=0))
+
+    def own_edges(i, carry):
+        use_edges(i)
+        return carry
+
+    with jax.named_scope("receive"):
+        lax.fori_loop(0, 4, receive, 0)
+    with jax.named_scope("own_edges"):
+        lax.fori_loop(0, 1, own_edges, 0)
 
     def far_edges(i, carry):
         with jax.named_scope("wait_edges"):

time: 62.6 us -> 62.6 us (level)
  no operation moved by 1% of the time
where the time goes in v4:
time: 62.6 us; the launch traced here: 62.5 us
  Pallas kernels  61.7 us (99%)
  local copies, waits for them, and re-layouts  0.8 us (1%)
    pallas_call x1, Pallas kernels, shards(): pl.pallas_call(functools.partial(kernel, count), out_shape=pltpu.VMEM((ro...  61.7 us

profile of v4, /device:TPU:513, one launch (start us, length us, event | category | flops | bytes accessed | tf_op | source)
XLA Modules:
  0.0 62.5 jit_solution(4919358298327288150)
XLA Ops:
  0.0 61.7 %encode_attend.1 = bf16[512,512]{1,0:T(8,128)(2,1)S(1)} custom-call(bf16[1024,512]{1,0:T(8,128)(2,1)} %grid_hbm.1, bf16[512,512]{1,0:T(8,128)(2,1)} %mesh_hbm.1, s32[20,128]{1,0:T(8,128)} %send_hbm.1, s32[20,128]{1,0:T(8,128)} %recv_hbm.1, s32[32,512]{1,0:T(8,128)} %bitcast.4, bf16[512,512]{1,0:T(8,128)(2,1)} %grid_w_hbm.1, f32[1,512]{1,0:T(1,128)} %bitcast.5, ...), custom_call_target="tpu_custom_call" | custom-call | tf_op jit(solution)/shard_map/encode_attend/pallas_call | solution.py:476
  61.7 0.8 %copy.22 = bf16[512,512]{1,0:T(8,128)(2,1)} copy(bf16[512,512]{1,0:T(8,128)(2,1)S(1)} %encode_attend.1) | data formatting | bytes 1048576

commit v5 on v4

--- a/solution.py
+++ b/solution.py
@@ -379,9 +379,10 @@
 
     def wait_nodes(blocks):
         for role, q in blocks:
-            arrived(NODE_SLOT[(role, q)])
-            if role == FW:
-                pass_on(q).start()
+            if role != FW:
+                arrived(NODE_SLOT[(role, q)])
+
+    passed = {0: (0, 1), 1: (2,), 2: (3,)}
 
     def attend(block, pairs):
         size = 2 * pairs * LANES
@@ -415,6 +416,9 @@
             for index in range(6):
                 @pl.when(i == index)
                 def _():
+                    for q in passed.get(index, ()):
+                        arrived(NODE_SLOT[(FW, q)])
+                        pass_on(q).start()
                     wait_nodes(NODE_USE[8 + 2 * index : 10 + 2 * index])
 
         with jax.named_scope("attend_two"):

time: 62.6 us -> 62.2 us (level)
  no operation moved by 1% of the time
where the time goes in v5:
time: 62.2 us; the launch traced here: 62 us
  Pallas kernels  61.2 us (98%)
  local copies, waits for them, and re-layouts  0.8 us (1%)
    pallas_call x1, Pallas kernels, shards(): pl.pallas_call(functools.partial(kernel, count), out_shape=pltpu.VMEM((ro...  61.2 us

profile of v5, /device:TPU:513, one launch (start us, length us, event | category | flops | bytes accessed | tf_op | source)
XLA Modules:
  0.0 62.0 jit_solution(14240175930205649668)
XLA Ops:
  0.0 61.2 %encode_attend.1 = bf16[512,512]{1,0:T(8,128)(2,1)S(1)} custom-call(bf16[1024,512]{1,0:T(8,128)(2,1)} %grid_hbm.1, bf16[512,512]{1,0:T(8,128)(2,1)} %mesh_hbm.1, s32[20,128]{1,0:T(8,128)} %send_hbm.1, s32[20,128]{1,0:T(8,128)} %recv_hbm.1, s32[32,512]{1,0:T(8,128)} %bitcast.4, bf16[512,512]{1,0:T(8,128)(2,1)} %grid_w_hbm.1, f32[1,512]{1,0:T(1,128)} %bitcast.5, ...), custom_call_target="tpu_custom_call" | custom-call | tf_op jit(solution)/shard_map/encode_attend/pallas_call | solution.py:480
  61.2 0.8 %copy.22 = bf16[512,512]{1,0:T(8,128)(2,1)} copy(bf16[512,512]{1,0:T(8,128)(2,1)S(1)} %encode_attend.1) | data formatting | bytes 1048576
